TPU v7x, 32 devices: a whole 2x2x4 slice. The times are simulated.
32 devices in a mesh: face: 4 (over x, core), sub: 8 (over z, y).
Axes of the slice: x: 2, y: 2, z: 4, core: 2. Of those that a mesh axis runs over, the one named last changes fastest.
Arguments:
- grid_latent: bfloat16 [16384, 512], P(('face', 'sub')), may hold values from -6 to 6
- mesh_latent: bfloat16 [4096, 512], P(('face', 'sub')), may hold values from -6 to 6
- edge_latent: bfloat16 [32768, 512], P(('face', 'sub')), may hold values from -6 to 6
- mesh_cotangent: bfloat16 [4096, 512], P(('face', 'sub')), may hold values from -6 to 6
- edge_cotangent: bfloat16 [32768, 512], P(('face', 'sub')), may hold values from -6 to 6
- grid_send: int32 [32, 4, 256], P(('face', 'sub')), may hold values from 0 to 511
- grid_slot: int32 [32768], P(('face', 'sub')), may hold values from 0 to 1535, as said below
- grid_target: int32 [32768], P(('face', 'sub')), may hold values from 0 to 127
- mesh_halo: int32 [32, 4, 64], P(('face', 'sub')), may hold values from 0 to 127
- mesh_send: int32 [32, 32, 4], P(('face', 'sub')), may hold values from 0 to 127
- mesh_slot: int32 [32768], P(('face', 'sub')), may hold values from 0 to 511, as said below
- mesh_target: int32 [32768], P(('face', 'sub')), may hold values from 0 to 127
- weights: bfloat16 [10, 512, 512], replicated, may hold values from -0.25 to 0.25
Outputs:
- mesh_update: bfloat16 [4096, 512], P(('face', 'sub'))
- grid_grad: bfloat16 [16384, 512], P(('face', 'sub'))
- mesh_grad: bfloat16 [4096, 512], P(('face', 'sub'))
- edge_grad: bfloat16 [32768, 512], P(('face', 'sub'))
- weight_grads: bfloat16 [10, 512, 512], replicated
Inputs may be any that keep to these rules, and one draw needn't show every extreme that they name: grid_slot[e] names the edge device's own 512 grid rows or, above them, the 256 rows listed by each of its four neighbours in direction order. grid_target[e] is local to the edge's device. grid_send[q, k] lists local rows of device q for the device d with nb(d, k) = q; a row may appear in several slots. mesh_slot[e] names the own 128 mesh rows, then the 64 rows listed by each of the four neighbours, then 4 far rows from each device, source major. mesh_target[e] is local to the edge's device. mesh_halo[q, k] lists local rows of device q for its neighbour in direction k. mesh_send[q, d] lists local rows of device q for far edges of device d.
All inputs are finite; a program needn't handle non-finite values.
Results may differ from a plain program's by a relative error of at most 0.016.
Values may be sent and summed in bfloat16 or wider, within the bound.
A program may use at most 128 MiB of HBM per device.

v0:
```python
import jax
import jax.numpy as jnp
from jax import lax
from jax.sharding import PartitionSpec as P

norm_eps = 1e-05


def shifted(value, axis, steps):
    count = lax.axis_size(axis)
    pairs = [(source, (source + steps) % count) for source in range(count)]
    return lax.ppermute(value, axis, pairs)


def layer_norm(values):
    centre = values - jnp.mean(values, axis=-1, keepdims=True)
    spread = jnp.mean(centre * centre, axis=-1, keepdims=True)
    return centre * lax.rsqrt(spread + norm_eps)


def layer_norm_back(values, upstream):
    centre = values - jnp.mean(values, axis=-1, keepdims=True)
    inverse = lax.rsqrt(jnp.mean(centre * centre, axis=-1, keepdims=True) + norm_eps)
    normed = centre * inverse
    return inverse * (
        upstream
        - jnp.mean(upstream, axis=-1, keepdims=True)
        - normed * jnp.mean(upstream * normed, axis=-1, keepdims=True)
    )


def swish_slope(values):
    sigmoid_values = jax.nn.sigmoid(values)
    return sigmoid_values * (1.0 + values * (1.0 - sigmoid_values))


def product(former, latter):
    return jnp.dot(former, latter, preferred_element_type=jnp.float32)


def outer_sum(former, latter):
    return lax.dot_general(
        former, latter, (((0,), (0,)), ((), ())), preferred_element_type=jnp.float32
    )


def back_product(former, latter):
    return lax.dot_general(
        former, latter, (((1,), (1,)), ((), ())), preferred_element_type=jnp.float32
    )


def select_columns(ids, count):
    columns = lax.broadcasted_iota(jnp.int32, (ids.shape[0], count), 1)
    return (ids[:, None] == columns).astype(jnp.bfloat16)


def select_pair(ids, others, count, other_count):
    columns = lax.broadcasted_iota(jnp.int32, (ids.shape[0], count + other_count), 1)
    hit = (ids[:, None] == columns) | ((others + count)[:, None] == columns)
    return hit.astype(jnp.bfloat16)


def stack_grads(terms):
    return jnp.stack([term.astype(jnp.bfloat16) for term in terms])


def grid_neighbours(outgoing):
    from_sub = [shifted(outgoing[block], "sub", offset) for block, offset in ((0, 1), (1, -1))]
    from_face = [shifted(outgoing[block], "face", offset) for block, offset in ((2, 1), (3, -1))]
    return jnp.concatenate(from_sub + from_face, axis=0)


def grid_returns(partials):
    to_sub = [shifted(partials[block], "sub", offset) for block, offset in ((0, -1), (1, 1))]
    to_face = [shifted(partials[block], "face", offset) for block, offset in ((2, -1), (3, 1))]
    return jnp.concatenate(to_sub + to_face, axis=0)


def mesh_neighbours(outgoing):
    from_sub = [shifted(outgoing[block], "sub", offset) for block, offset in ((0, 1), (1, -1))]
    from_face = [shifted(outgoing[block], "face", offset) for block, offset in ((2, 1), (3, -1))]
    return jnp.concatenate(from_sub + from_face, axis=0)


def mesh_returns(partials):
    to_sub = [shifted(partials[block], "sub", offset) for block, offset in ((0, -1), (1, 1))]
    to_face = [shifted(partials[block], "face", offset) for block, offset in ((2, -1), (3, 1))]
    return jnp.concatenate(to_sub + to_face, axis=0)


def move_mesh(outgoing):
    return lax.all_to_all(outgoing, ("face", "sub"), split_axis=0, concat_axis=0, tiled=True)


def return_mesh(outgoing):
    return lax.all_to_all(outgoing, ("face", "sub"), split_axis=0, concat_axis=0, tiled=True)


def on_device(
    grid_latent,
    mesh_latent,
    edge_latent,
    mesh_cotangent,
    edge_cotangent,
    grid_send,
    grid_slot,
    grid_target,
    mesh_halo,
    mesh_send,
    mesh_slot,
    mesh_target,
    weights,
):
    peer_count = lax.axis_size("face") * lax.axis_size("sub")
    latent = weights.shape[1]
    mesh_rows = mesh_latent.shape[0]
    grid_rows = grid_latent.shape[0]
    grid_table = grid_send[0].reshape(-1)
    halo_table = mesh_halo[0].reshape(-1)
    far_table = mesh_send[0].reshape(-1)
    halo_count = halo_table.shape[0]
    slot_count = mesh_rows + halo_count + far_table.shape[0]
    grid_slot_count = grid_rows + grid_table.shape[0]
    pick_grid = select_columns(grid_table, grid_rows)
    pick_halo_far = select_columns(jnp.concatenate([halo_table, far_table]), mesh_rows)
    grid_pair = select_pair(grid_slot, grid_target, grid_slot_count, mesh_rows)
    mesh_pair = select_pair(mesh_slot, mesh_target, slot_count, mesh_rows)
    grid_onehot = select_columns(grid_target, mesh_rows)
    mesh_onehot = select_columns(mesh_target, mesh_rows)
    encode_scale = 1.0 / (grid_slot.shape[0] * peer_count) ** 0.5
    process_scale = 1.0 / (mesh_slot.shape[0] * peer_count) ** 0.5
    update_scale = 1.0 / (mesh_rows * peer_count) ** 0.5
    grid_project = product(grid_latent, weights[0]).astype(jnp.bfloat16)
    grid_outgoing = product(pick_grid, grid_project).astype(jnp.bfloat16).reshape(4, -1, latent)
    encode_receive = product(mesh_latent, weights[1]).astype(jnp.bfloat16)
    grid_source = jnp.concatenate(
        [grid_project, grid_neighbours(grid_outgoing), encode_receive], axis=0
    )
    encoder_pre = product(grid_pair, grid_source)
    encoder_hidden = jax.nn.silu(encoder_pre).astype(jnp.bfloat16)
    encoder_linear = product(encoder_hidden, weights[2])
    encoder_message = layer_norm(encoder_linear).astype(jnp.bfloat16)
    encoder_total = outer_sum(grid_onehot, encoder_message)
    mesh_middle = (mesh_latent.astype(jnp.float32) + encoder_total).astype(jnp.bfloat16)
    sender_rows = product(mesh_middle, weights[4]).astype(jnp.bfloat16)
    outgoing = product(pick_halo_far, sender_rows).astype(jnp.bfloat16)
    halo_outgoing = outgoing[:halo_count].reshape(4, -1, latent)
    far_outgoing = outgoing[halo_count:].reshape(peer_count, -1, latent)
    far_incoming = move_mesh(far_outgoing).reshape(-1, latent)
    process_receive = product(mesh_middle, weights[5]).astype(jnp.bfloat16)
    mesh_source = jnp.concatenate(
        [sender_rows, mesh_neighbours(halo_outgoing), far_incoming, process_receive], axis=0
    )
    process_pre = product(edge_latent, weights[3]) + product(mesh_pair, mesh_source)
    process_hidden = jax.nn.silu(process_pre).astype(jnp.bfloat16)
    process_linear = product(process_hidden, weights[6])
    edge_update = layer_norm(process_linear).astype(jnp.bfloat16)
    process_round = outer_sum(mesh_onehot, edge_update).astype(jnp.bfloat16)
    update_pre = product(mesh_middle, weights[7]) + product(process_round, weights[8])
    update_hidden = jax.nn.silu(update_pre).astype(jnp.bfloat16)
    update_linear = product(update_hidden, weights[9])
    mesh_update = (mesh_middle.astype(jnp.float32) + layer_norm(update_linear)).astype(jnp.bfloat16)
    outer_cot = mesh_cotangent.astype(jnp.float32)
    cot_linear = layer_norm_back(update_linear, outer_cot).astype(jnp.bfloat16)
    grad_update_output = outer_sum(update_hidden, cot_linear)
    cot_update = (back_product(cot_linear, weights[9]) * swish_slope(update_pre)).astype(
        jnp.bfloat16
    )
    grad_update_self = outer_sum(mesh_middle, cot_update)
    grad_update_message = outer_sum(process_round, cot_update)
    cot_total = back_product(cot_update, weights[8]).astype(jnp.bfloat16)
    edge_cot = edge_cotangent.astype(jnp.float32)
    cot_edge = product(mesh_onehot, cot_total) + edge_cot
    cot_plinear = layer_norm_back(process_linear, cot_edge).astype(jnp.bfloat16)
    grad_process_output = outer_sum(process_hidden, cot_plinear)
    cot_process = back_product(cot_plinear, weights[6]) * swish_slope(process_pre)
    cot_round = cot_process.astype(jnp.bfloat16)
    grad_process_edge = outer_sum(edge_latent, cot_round)
    edge_grad = (edge_cot + back_product(cot_round, weights[3])).astype(jnp.bfloat16)
    cot_slot = outer_sum(mesh_pair, cot_round)
    cot_receive = cot_slot[slot_count:].astype(jnp.bfloat16)
    grad_process_receiver = outer_sum(mesh_middle, cot_receive)
    halo_partials = (
        cot_slot[mesh_rows : mesh_rows + halo_count].astype(jnp.bfloat16).reshape(4, -1, latent)
    )
    far_partials = (
        cot_slot[mesh_rows + halo_count : slot_count]
        .astype(jnp.bfloat16)
        .reshape(peer_count, -1, latent)
    )
    far_returned = return_mesh(far_partials).reshape(-1, latent)
    returned = jnp.concatenate([mesh_returns(halo_partials), far_returned], axis=0)
    sender_total = cot_slot[:mesh_rows] + outer_sum(pick_halo_far, returned)
    cot_sender = sender_total.astype(jnp.bfloat16)
    grad_process_sender = outer_sum(mesh_middle, cot_sender)
    cot_middle = (
        outer_cot
        + back_product(cot_update, weights[7])
        + back_product(cot_receive, weights[5])
        + back_product(cot_sender, weights[4])
    )
    process_grads = stack_grads(
        [
            grad_process_edge,
            grad_process_sender,
            grad_process_receiver,
            grad_process_output,
            grad_update_self,
            grad_update_message,
            grad_update_output,
        ]
    )
    process_grads = lax.psum(process_grads, ("face", "sub"))
    cot_message = product(grid_onehot, cot_middle.astype(jnp.bfloat16))
    cot_elinear = layer_norm_back(encoder_linear, cot_message).astype(jnp.bfloat16)
    grad_encode_output = outer_sum(encoder_hidden, cot_elinear)
    cot_encoder = back_product(cot_elinear, weights[2]) * swish_slope(encoder_pre)
    cot_gslot = outer_sum(grid_pair, cot_encoder.astype(jnp.bfloat16))
    cot_mesh_receive = cot_gslot[grid_slot_count:].astype(jnp.bfloat16)
    grad_encode_receiver = outer_sum(mesh_latent, cot_mesh_receive)
    mesh_grad = (cot_middle + back_product(cot_mesh_receive, weights[1])).astype(jnp.bfloat16)
    grid_partials = cot_gslot[grid_rows:grid_slot_count].astype(jnp.bfloat16).reshape(4, -1, latent)
    grid_returned = grid_returns(grid_partials)
    cot_grid = (cot_gslot[:grid_rows] + outer_sum(pick_grid, grid_returned)).astype(jnp.bfloat16)
    grad_encode_sender = outer_sum(grid_latent, cot_grid)
    grid_grad = back_product(cot_grid, weights[0]).astype(jnp.bfloat16)
    encode_grads = stack_grads([grad_encode_sender, grad_encode_receiver, grad_encode_output])
    encode_grads, process_grads = lax.optimization_barrier((encode_grads, process_grads))
    encode_grads = lax.psum(encode_grads, ("face", "sub"))
    summed = jnp.concatenate([encode_grads, process_grads], axis=0).astype(jnp.float32)
    scale_column = jnp.array(
        [encode_scale] * 3 + [process_scale] * 4 + [update_scale] * 3, jnp.float32
    )
    weight_grads = (summed * scale_column[:, None, None]).astype(jnp.bfloat16)
    return (mesh_update, grid_grad, mesh_grad, edge_grad, weight_grads)


def solution(mesh):
    return jax.shard_map(
        on_device,
        mesh=mesh,
        in_specs=(
            P(("face", "sub"), None),
            P(("face", "sub"), None),
            P(("face", "sub"), None),
            P(("face", "sub"), None),
            P(("face", "sub"), None),
            P(("face", "sub"), None, None),
            P(("face", "sub")),
            P(("face", "sub")),
            P(("face", "sub"), None, None),
            P(("face", "sub"), None, None),
            P(("face", "sub")),
            P(("face", "sub")),
            P(),
        ),
        out_specs=(
            P(("face", "sub"), None),
            P(("face", "sub"), None),
            P(("face", "sub"), None),
            P(("face", "sub"), None),
            P(),
        ),
        check_vma=False,
    )
```

profile of v0, /device:TPU:0, one launch (start us, length us, event | category | flops | bytes accessed | tf_op | source)
XLA Modules:
  0.0 431.3 jit_solution(9846801557097275770)
XLA Ops:
  8.0 2.5 constant_dynamic-update-slice_fusion.4
  12.2 2.5 collective-permute-start.3
  14.7 4.6 %collective-permute-start.1 = (bf16[256,512]{1,0:T(8,128)(2,1)}, bf16[256,512]{1,0:T(8,128)(2,1)S(1)}, u32[]{:S(2)}, u32[]{:S(2)}) collective-permute-start(bf16[256,512]{1,0:T(8,128)(2,1)} %get-tuple-element.31), channel_id=1, source_target_pairs={{0,7},{1,0},{2,1},{3,2},{4,3},{5,4},{6,5},{7,6},{8,15},{9,8},{10,9... | collective-permute-start | bytes 786440 | tf_op jit(solution)/shard_map/ppermute | solution.py:12
  19.2 3.1 fusion.81
  24.0 6.8 %collective-permute-done = bf16[256,512]{1,0:T(8,128)(2,1)S(1)} collective-permute-done((bf16[256,512]{1,0:T(8,128)(2,1)}, bf16[256,512]{1,0:T(8,128)(2,1)S(1)}, u32[]{:S(2)}, u32[]{:S(2)}) %collective-permute-start) | collective-permute-done | bytes 262176 | tf_op jit(solution)/shard_map/ppermute | solution.py:12
  35.6 3.6 fusion.3
  39.2 2.3 fusion.146
  50.1 5.0 %all-to-all-start = ((bf16[32,4,512]{2,1,0:T(4,128)(2,1)}), bf16[32,4,512]{2,1,0:T(4,128)(2,1)}, u32[]{:S(2)}, u32[]{:S(2)}) async-start(bf16[32,4,512]{2,1,0:T(4,128)(2,1)} %reshape.127), calls=%async_computation | async-start | bytes 262144 | tf_op jit(solution)/shard_map/all_to_all | solution.py:93
  56.6 4.3 collective-permute-start.5
  70.4 3.0 fusion.17
  73.3 2.3 fusion.147
  82.4 2.1 convolution_add_fusion.4
  84.5 4.3 %fusion.141 = (f32[1024]{0:T(1024)S(1)}, f32[1024]{0:T(1024)S(1)}, f32[1024,512]{0,1:T(8,128)}) fusion(f32[1024]{0:T(1024)S(1)} %add_rsqrt_fusion, f32[1024,512]{0,1:T(8,128)} %copy-done.2, f32[1024]{0:T(1024)S(1)} %broadcast_multiply_fusion.4, bf16[1024,512]{0,1:T(8,128)(2,1)} %copy.32, bf16[128,512]{1,0:T(8,128)(2,1)S(1)} %fusion.46, ...), kind=kOutput, calls=%fused_computation.216 | convolution fusion | flops 205191168 | bytes 5918720 | tf_op jit(solution)/shard_map/dot_general | solution.py:38
  88.9 2.9 multiply_convert_fusion.4
  91.9 2.7 multiply_convert_fusion.3
  94.6 2.6 fusion.151
  98.7 5.1 %collective-permute-start.8 = (bf16[64,512]{1,0:T(8,128)(2,1)S(1)}, bf16[64,512]{1,0:T(8,128)(2,1)S(1)}, u32[]{:S(2)}, u32[]{:S(2)}) collective-permute-start(bf16[64,512]{1,0:T(8,128)(2,1)S(1)} %get-tuple-element.36), channel_id=1, source_target_pairs={{0,7},{1,0},{2,1},{3,2},{4,3},{5,4},{6,5},{7,6},{8,15},{9,8},{10,9... | collective-permute-start | bytes 196616 | tf_op jit(solution)/shard_map/ppermute | solution.py:12
  106.0 2.6 all-to-all-start.1
  112.1 5.6 %collective-permute-done.9 = bf16[64,512]{1,0:T(8,128)(2,1)S(1)} collective-permute-done((bf16[64,512]{1,0:T(8,128)(2,1)S(1)}, bf16[64,512]{1,0:T(8,128)(2,1)S(1)}, u32[]{:S(2)}, u32[]{:S(2)}) %collective-permute-start.9) | collective-permute-done | bytes 65568 | tf_op jit(solution)/shard_map/ppermute | solution.py:12
  123.6 2.0 fusion.38
  131.0 2.1 multiply_convert_fusion.2
  133.2 6.9 %fusion.152 = (bf16[1664,512]{1,0:T(8,128)(2,1)S(1)}, f32[1664,512]{1,0:T(8,128)}) fusion(f32[1024,512]{1,0:T(8,128)} %copy-done.55, bf16[1024,512]{0,1:T(8,128)(2,1)S(1)} %multiply_convert_fusion.2, bf16[10,512,512]{2,1,0:T(8,128)(2,1)} %param.26, s32[1024]{0:T(1024)S(1)} %copy-done.32, s32[1024]{0:T(1024)S(1)} %copy-done.50), kind=kOutput, calls=%fused_computation.225 | convolution fusion | flops 2292383744 | bytes 8790016 | tf_op jit(solution)/shard_map/dot_general | solution.py:42
  145.2 8.8 %collective-permute-done.12 = bf16[256,512]{1,0:T(8,128)(2,1)S(1)} collective-permute-done((bf16[256,512]{1,0:T(8,128)(2,1)S(1)}, bf16[256,512]{1,0:T(8,128)(2,1)S(1)}, u32[]{:S(2)}, u32[]{:S(2)}) %collective-permute-start.12) | collective-permute-done | bytes 262176 | tf_op jit(solution)/shard_map/ppermute | solution.py:12
  154.0 5.5 %collective-permute-done.13 = bf16[256,512]{1,0:T(8,128)(2,1)S(1)} collective-permute-done((bf16[256,512]{1,0:T(8,128)(2,1)S(1)}, bf16[256,512]{1,0:T(8,128)(2,1)S(1)}, u32[]{:S(2)}, u32[]{:S(2)}) %collective-permute-start.13) | collective-permute-done | bytes 262176 | tf_op jit(solution)/shard_map/ppermute | solution.py:12
  159.5 2.3 fusion.28
  163.6 109.1 %all-reduce.3.cloned.1.call-done = bf16[7,512,512]{1,2,0:T(8,128)(2,1)} async-done(((bf16[7,512,512]{1,2,0:T(8,128)(2,1)}), bf16[7,512,512]{1,2,0:T(8,128)(2,1)}) %all-reduce.3.cloned.1.call-update) | async-done | bytes 3670032 | tf_op jit(solution)/shard_map/psum | solution.py:214
  272.7 2.1 fusion.10
  276.1 2.1 fusion.48
  278.2 2.3 convolution_convert_fusion.1
  280.5 129.4 %all-reduce.5.cloned.1.call-done = bf16[3,512,512]{1,2,0:T(8,128)(2,1)} async-done(((bf16[3,512,512]{1,2,0:T(8,128)(2,1)}), bf16[3,512,512]{1,2,0:T(8,128)(2,1)}) %all-reduce.5.cloned.1.call-update) | async-done | bytes 1572880 | tf_op jit(solution)/shard_map/psum | solution.py:230
  409.9 6.5 %multiply_convert_fusion = bf16[10,512,512]{1,2,0:T(8,128)(2,1)} fusion(bf16[7,512,512]{1,2,0:T(8,128)(2,1)} %all-reduce.3.cloned.1.call-done, bf16[3,512,512]{1,2,0:T(8,128)(2,1)} %all-reduce.5.cloned.1.call-done, f32[10]{0:T(128)S(1)} %copy-done.45), kind=kLoop, calls=%fused_computation | loop fusion | flops 10485760 | bytes 10485800 | tf_op jit(solution)/shard_map/convert_element_type | solution.py:235
  416.4 8.0 %copy.42 = bf16[10,512,512]{2,1,0:T(8,128)(2,1)} copy(bf16[10,512,512]{1,2,0:T(8,128)(2,1)} %multiply_convert_fusion) | data formatting | bytes 10485760
  (217 shorter events, 61.6 us)
Async XLA Ops:
  7.2 12.1 %copy-start = (bf16[1024,512]{1,0:T(8,128)(2,1)S(1)}, bf16[1024,512]{1,0:T(8,128)(2,1)}, u32[]{:S(2)}) copy-start(bf16[1024,512]{1,0:T(8,128)(2,1)} %param.16) | copy-start | bytes 3145732
  12.2 20.8 %collective-permute-start.3 = (bf16[256,512]{1,0:T(8,128)(2,1)}, bf16[256,512]{1,0:T(8,128)(2,1)S(1)}, u32[]{:S(2)}, u32[]{:S(2)}) collective-permute-start(bf16[256,512]{1,0:T(8,128)(2,1)} %get-tuple-element.29), channel_id=1, source_target_pairs={{0,24},{8,0},{16,8},{24,16},{1,25},{9,1},{17,9},{25,17},{2,26},{10... | collective-permute-start | bytes 786440 | tf_op jit(solution)/shard_map/ppermute | solution.py:12
  14.7 17.6 %collective-permute-start.2 = (bf16[256,512]{1,0:T(8,128)(2,1)}, bf16[256,512]{1,0:T(8,128)(2,1)S(1)}, u32[]{:S(2)}, u32[]{:S(2)}) collective-permute-start(bf16[256,512]{1,0:T(8,128)(2,1)} %get-tuple-element.30), channel_id=1, source_target_pairs={{0,8},{8,16},{16,24},{24,0},{1,9},{9,17},{17,25},{25,1},{2,10},{10... | collective-permute-start | bytes 786440 | tf_op jit(solution)/shard_map/ppermute | solution.py:12
  14.7 16.9 %collective-permute-start.1 = (bf16[256,512]{1,0:T(8,128)(2,1)}, bf16[256,512]{1,0:T(8,128)(2,1)S(1)}, u32[]{:S(2)}, u32[]{:S(2)}) collective-permute-start(bf16[256,512]{1,0:T(8,128)(2,1)} %get-tuple-element.31), channel_id=1, source_target_pairs={{0,7},{1,0},{2,1},{3,2},{4,3},{5,4},{6,5},{7,6},{8,15},{9,8},{10,9... | collective-permute-start | bytes 786440 | tf_op jit(solution)/shard_map/ppermute | solution.py:12
  19.2 11.6 %collective-permute-start = (bf16[256,512]{1,0:T(8,128)(2,1)}, bf16[256,512]{1,0:T(8,128)(2,1)S(1)}, u32[]{:S(2)}, u32[]{:S(2)}) collective-permute-start(bf16[256,512]{1,0:T(8,128)(2,1)} %get-tuple-element.32), channel_id=1, source_target_pairs={{0,1},{1,2},{2,3},{3,4},{4,5},{5,6},{6,7},{7,0},{8,9},{9,10},{10,1... | collective-permute-start | bytes 786440 | tf_op jit(solution)/shard_map/ppermute | solution.py:12
  19.2 16.4 %copy-start.31 = (s32[1024]{0:T(1024)}, s32[1024]{0:T(1024)S(1)}, u32[]{:S(2)}) copy-start(s32[1024]{0:T(1024)S(1)} %broadcast_add_fusion.1) | copy-start | bytes 12292
  22.3 48.0 %copy-start.33 = (s32[1024]{0:T(1024)}, s32[1024]{0:T(1024)S(1)}, u32[]{:S(2)}) copy-start(s32[1024]{0:T(1024)S(1)} %broadcast_add_fusion) | copy-start | bytes 12292
  22.6 21.9 %copy-start.27 = (s32[384]{0:T(512)}, s32[384]{0:T(512)S(1)}, u32[]{:S(2)}) copy-start(s32[384]{0:T(512)S(1)} %pad_add_fusion) | copy-start | bytes 4612
  22.6 11.0 %copy-start.16 = (bf16[128,512]{1,0:T(8,128)(2,1)S(1)}, bf16[128,512]{1,0:T(8,128)(2,1)}, u32[]{:S(2)}) copy-start(bf16[128,512]{1,0:T(8,128)(2,1)} %param.15) | copy-start | bytes 393220
  22.7 13.0 %copy-start.49 = (s32[1024]{0:T(1024)S(1)}, s32[1024]{0:T(1024)}, u32[]{:S(2)}) copy-start(s32[1024]{0:T(1024)} %param.20) | copy-start | bytes 12292
  44.8 25.5 %copy-start.47 = (s32[1024]{0:T(1024)S(1)}, s32[1024]{0:T(1024)}, u32[]{:S(2)}) copy-start(s32[1024]{0:T(1024)} %param.24) | copy-start | bytes 12292
  45.5 15.3 %collective-permute-start.4 = (bf16[64,512]{1,0:T(8,128)(2,1)}, bf16[64,512]{1,0:T(8,128)(2,1)}, u32[]{:S(2)}, u32[]{:S(2)}) collective-permute-start(bf16[64,512]{1,0:T(8,128)(2,1)} %get-tuple-element.40), channel_id=1, source_target_pairs={{0,1},{1,2},{2,3},{3,4},{4,5},{5,6},{6,7},{7,0},{8,9},{9,10},{10,1... | collective-permute-start | bytes 196616 | tf_op jit(solution)/shard_map/ppermute | solution.py:12
  50.1 15.1 %all-to-all-start = ((bf16[32,4,512]{2,1,0:T(4,128)(2,1)}), bf16[32,4,512]{2,1,0:T(4,128)(2,1)}, u32[]{:S(2)}, u32[]{:S(2)}) async-start(bf16[32,4,512]{2,1,0:T(4,128)(2,1)} %reshape.127), calls=%async_computation | async-start | bytes 262144 | tf_op jit(solution)/shard_map/all_to_all | solution.py:93
  55.1 9.5 %collective-permute-start.7 = (bf16[64,512]{1,0:T(8,128)(2,1)}, bf16[64,512]{1,0:T(8,128)(2,1)S(1)}, u32[]{:S(2)}, u32[]{:S(2)}) collective-permute-start(bf16[64,512]{1,0:T(8,128)(2,1)} %get-tuple-element.37), channel_id=1, source_target_pairs={{0,24},{8,0},{16,8},{24,16},{1,25},{9,1},{17,9},{25,17},{2,26},{10... | collective-permute-start | bytes 196616 | tf_op jit(solution)/shard_map/ppermute | solution.py:12
  56.6 7.4 %collective-permute-start.6 = (bf16[64,512]{1,0:T(8,128)(2,1)}, bf16[64,512]{1,0:T(8,128)(2,1)S(1)}, u32[]{:S(2)}, u32[]{:S(2)}) collective-permute-start(bf16[64,512]{1,0:T(8,128)(2,1)} %get-tuple-element.38), channel_id=1, source_target_pairs={{0,8},{8,16},{16,24},{24,0},{1,9},{9,17},{17,25},{25,1},{2,10},{10... | collective-permute-start | bytes 196616 | tf_op jit(solution)/shard_map/ppermute | solution.py:12
  56.6 6.8 %collective-permute-start.5 = (bf16[64,512]{1,0:T(8,128)(2,1)}, bf16[64,512]{1,0:T(8,128)(2,1)S(1)}, u32[]{:S(2)}, u32[]{:S(2)}) collective-permute-start(bf16[64,512]{1,0:T(8,128)(2,1)} %get-tuple-element.39), channel_id=1, source_target_pairs={{0,7},{1,0},{2,1},{3,2},{4,3},{5,4},{6,5},{7,6},{8,15},{9,8},{10,9... | collective-permute-start | bytes 196616 | tf_op jit(solution)/shard_map/ppermute | solution.py:12
  98.7 19.1 %copy-start.28 = (s32[384]{0:T(512)S(1)}, s32[384]{0:T(512)}, u32[]{:S(2)}) copy-start(s32[384]{0:T(512)} %copy-done.27) | copy-start | bytes 4612
  98.7 13.3 %collective-permute-start.8 = (bf16[64,512]{1,0:T(8,128)(2,1)S(1)}, bf16[64,512]{1,0:T(8,128)(2,1)S(1)}, u32[]{:S(2)}, u32[]{:S(2)}) collective-permute-start(bf16[64,512]{1,0:T(8,128)(2,1)S(1)} %get-tuple-element.36), channel_id=1, source_target_pairs={{0,7},{1,0},{2,1},{3,2},{4,3},{5,4},{6,5},{7,6},{8,15},{9,8},{10,9... | collective-permute-start | bytes 196616 | tf_op jit(solution)/shard_map/ppermute | solution.py:12
  105.2 15.2 %copy-start.26 = (s32[1024]{0:T(1024)S(1)}, s32[1024]{0:T(1024)}, u32[]{:S(2)}) copy-start(s32[1024]{0:T(1024)} %param.21) | copy-start | bytes 12292
  106.0 11.8 %all-to-all-start.1 = ((bf16[32,4,512]{2,1,0:T(4,128)(2,1)}), bf16[32,4,512]{2,1,0:T(4,128)(2,1)S(1)}, u32[]{:S(2)}, u32[]{:S(2)}) async-start(bf16[32,4,512]{2,1,0:T(4,128)(2,1)} %reshape.129), calls=%async_computation.1 | async-start | bytes 262144 | tf_op jit(solution)/shard_map/all_to_all | solution.py:97
  108.5 164.1 %all-reduce.3.cloned.1.call-start = ((), (), s32[]{:S(2)}) async-start(), calls=%async_computation.2 | async-start | bytes 7340032 | tf_op jit(solution)/shard_map/psum | solution.py:214
  108.6 9.1 %collective-permute-start.11 = (bf16[64,512]{1,0:T(8,128)(2,1)S(1)}, bf16[64,512]{1,0:T(8,128)(2,1)S(1)}, u32[]{:S(2)}, u32[]{:S(2)}) collective-permute-start(bf16[64,512]{1,0:T(8,128)(2,1)S(1)} %get-tuple-element.33), channel_id=1, source_target_pairs={{0,8},{8,16},{16,24},{24,0},{1,9},{9,17},{17,25},{25,1},{2,10},{10... | collective-permute-start | bytes 196616 | tf_op jit(solution)/shard_map/ppermute | solution.py:12
  108.8 8.9 %collective-permute-start.10 = (bf16[64,512]{1,0:T(8,128)(2,1)S(1)}, bf16[64,512]{1,0:T(8,128)(2,1)S(1)}, u32[]{:S(2)}, u32[]{:S(2)}) collective-permute-start(bf16[64,512]{1,0:T(8,128)(2,1)S(1)} %get-tuple-element.34), channel_id=1, source_target_pairs={{0,24},{8,0},{16,8},{24,16},{1,25},{9,1},{17,9},{25,17},{2,26},{10... | collective-permute-start | bytes 196616 | tf_op jit(solution)/shard_map/ppermute | solution.py:12
  110.4 7.3 %collective-permute-start.9 = (bf16[64,512]{1,0:T(8,128)(2,1)S(1)}, bf16[64,512]{1,0:T(8,128)(2,1)S(1)}, u32[]{:S(2)}, u32[]{:S(2)}) collective-permute-start(bf16[64,512]{1,0:T(8,128)(2,1)S(1)} %get-tuple-element.35), channel_id=1, source_target_pairs={{0,1},{1,2},{2,3},{3,4},{4,5},{5,6},{6,7},{7,0},{8,9},{9,10},{10,1... | collective-permute-start | bytes 196616 | tf_op jit(solution)/shard_map/ppermute | solution.py:12
  130.9 279.0 %all-reduce.5.cloned.1.call-start = ((), (), s32[]{:S(2)}) async-start(), calls=%async_computation.3 | async-start | bytes 3145728 | tf_op jit(solution)/shard_map/psum | solution.py:230
  140.2 13.8 %collective-permute-start.12 = (bf16[256,512]{1,0:T(8,128)(2,1)S(1)}, bf16[256,512]{1,0:T(8,128)(2,1)S(1)}, u32[]{:S(2)}, u32[]{:S(2)}) collective-permute-start(bf16[256,512]{1,0:T(8,128)(2,1)S(1)} %get-tuple-element.25), channel_id=1, source_target_pairs={{0,7},{1,0},{2,1},{3,2},{4,3},{5,4},{6,5},{7,6},{8,15},{9,8},{10,9... | collective-permute-start | bytes 786440 | tf_op jit(solution)/shard_map/ppermute | solution.py:12
  141.6 12.4 %collective-permute-start.15 = (bf16[256,512]{1,0:T(8,128)(2,1)S(1)}, bf16[256,512]{1,0:T(8,128)(2,1)S(1)}, u32[]{:S(2)}, u32[]{:S(2)}) collective-permute-start(bf16[256,512]{1,0:T(8,128)(2,1)S(1)} %get-tuple-element.26), channel_id=1, source_target_pairs={{0,8},{8,16},{16,24},{24,0},{1,9},{9,17},{17,25},{25,1},{2,10},{10... | collective-permute-start | bytes 786440 | tf_op jit(solution)/shard_map/ppermute | solution.py:12
  141.6 12.4 %collective-permute-start.14 = (bf16[256,512]{1,0:T(8,128)(2,1)S(1)}, bf16[256,512]{1,0:T(8,128)(2,1)S(1)}, u32[]{:S(2)}, u32[]{:S(2)}) collective-permute-start(bf16[256,512]{1,0:T(8,128)(2,1)S(1)} %get-tuple-element.27), channel_id=1, source_target_pairs={{0,24},{8,0},{16,8},{24,16},{1,25},{9,1},{17,9},{25,17},{2,26},{10... | collective-permute-start | bytes 786440 | tf_op jit(solution)/shard_map/ppermute | solution.py:12
  143.4 16.1 %copy-start.30 = (s32[1,2,4,128]{3,1,2,0:T(2,128)S(1)}, s32[1,2,4,128]{3,1,2,0:T(2,128)}, u32[]{:S(2)}) copy-start(s32[1,2,4,128]{3,1,2,0:T(2,128)} %copy-done.29) | copy-start | bytes 12292
  143.4 16.1 %collective-permute-start.13 = (bf16[256,512]{1,0:T(8,128)(2,1)S(1)}, bf16[256,512]{1,0:T(8,128)(2,1)S(1)}, u32[]{:S(2)}, u32[]{:S(2)}) collective-permute-start(bf16[256,512]{1,0:T(8,128)(2,1)S(1)} %get-tuple-element.28), channel_id=1, source_target_pairs={{0,1},{1,2},{2,3},{3,4},{4,5},{5,6},{6,7},{7,0},{8,9},{9,10},{10,1... | collective-permute-start | bytes 786440 | tf_op jit(solution)/shard_map/ppermute | solution.py:12
  162.2 110.5 %copy-start.3 = (bf16[1024,512]{0,1:T(8,128)(2,1)S(1)}, bf16[1024,512]{0,1:T(8,128)(2,1)}, u32[]{:S(2)}) copy-start(bf16[1024,512]{0,1:T(8,128)(2,1)} %copy.32) | copy-start | bytes 3145732
  274.8 135.1 %copy-start.45 = (f32[10]{0:T(128)S(1)}, f32[10]{0:T(128)}, u32[]{:S(2)}) copy-start(f32[10]{0:T(128)} %constant.34.clone) | copy-start | bytes 124
  (45 other events, 202.0 us)
Sparse Core Ops, SparseCore 0:
  131.1 141.5 all-reduce.2
  278.0 131.9 all-reduce.4
where the time goes:
time: 433 us; the launch traced here: 431 us
  waiting for transfers between devices  266 us (61%)
  matrix products  75.1 us (17%)
  starting transfers between devices  33.9 us (8%)
  local copies, waits for them, and re-layouts  26.5 us (6%)
  between operations  14.9 us (3%)
  other arithmetic  14.6 us (3%)
    psum x1, waiting for transfers between devices, on_device(): encode_grads = lax.psum(encode_grads, ('face', 'sub'))  129 us
    psum x1, waiting for transfers between devices, on_device(): process_grads = lax.psum(process_grads, ('face', 'sub'))  109 us
    dot_general x16, matrix products, product(): return jnp.dot(former, latter, preferred_element_type=jnp.float32)  33.8 us
    ppermute x16, waiting for transfers between devices, shifted(): return lax.ppermute(value, axis, pairs)  27.7 us
    ppermute x16, starting transfers between devices, shifted(): return lax.ppermute(value, axis, pairs)  26.2 us
    dot_general x16, matrix products, outer_sum(): lax.dot_general(former, latter, (((0,), (0,)), ((), ())), preferred_eleme...  26 us
    unnamed x132, local copies, waits for them, and re-layouts  20 us
    dot_general x8, matrix products, back_product(): lax.dot_general(former, latter, (((1,), (1,)), ((), ())), preferred_eleme...  15.3 us
  transfers between devices with their start and end apart: 20, of which 7 were waited for; matrix products, arithmetic and copies ran while one was open for 9% of the time, Pallas kernels for 0%

commit v1 on v0

--- a/solution.py
+++ b/solution.py
@@ -227,7 +227,7 @@
     grid_grad = back_product(cot_grid, weights[0]).astype(jnp.bfloat16)
     encode_grads = stack_grads([grad_encode_sender, grad_encode_receiver, grad_encode_output])
     encode_grads, process_grads = lax.optimization_barrier((encode_grads, process_grads))
-    encode_grads = lax.psum(encode_grads, ("face", "sub"))
+    encode_grads = jnp.sum(lax.all_gather(encode_grads, ("face", "sub")), axis=0)
     summed = jnp.concatenate([encode_grads, process_grads], axis=0).astype(jnp.float32)
     scale_column = jnp.array(
         [encode_scale] * 3 + [process_scale] * 4 + [update_scale] * 3, jnp.float32

time: 433 us -> 590 us (1.36)
  waiting for transfers between devices: 266 us -> 405 us
  other arithmetic: 14.6 us -> 29.3 us
    all_gather x0 -> x1, waiting for transfers between devices: none -> 268 us  [on_device(): lax.all_gather(encode_grads, ('face', 'sub'))]
    psum x1 -> x0, waiting for transfers between devices: 129 us -> none  [on_device(): encode_grads = lax.psum(encode_grads, ('face', 'sub'))]
    reduce_sum x0 -> x1, other arithmetic: none -> 16.4 us  [on_device(): jnp.sum(lax.all_gather(encode_grads, ('face', 'sub')), axis=0)]
    unnamed x132 -> x136, local copies, waits for them, and re-layouts: 20 us -> 20.8 us
  transfers between devices with their start and end apart: 20 -> 20, of which waited for: 7 -> 7; matrix products, arithmetic and copies ran while one was open for 9% -> 6% of each run, Pallas kernels for 0% -> 0%
where the time goes in v1:
time: 590 us; the launch traced here: 588 us
  waiting for transfers between devices  405 us (69%)
  matrix products  76.1 us (13%)
  starting transfers between devices  33.9 us (6%)
  local copies, waits for them, and re-layouts  29.6 us (5%)
  other arithmetic  29.3 us (5%)
  between operations  15 us (3%)
    all_gather x1, waiting for transfers between devices, on_device(): lax.all_gather(encode_grads, ('face', 'sub'))  268 us
    psum x1, waiting for transfers between devices, on_device(): process_grads = lax.psum(process_grads, ('face', 'sub'))  109 us
    dot_general x16, matrix products, product(): return jnp.dot(former, latter, preferred_element_type=jnp.float32)  33.8 us
    dot_general x16, matrix products, outer_sum(): lax.dot_general(former, latter, (((0,), (0,)), ((), ())), preferred_eleme...  26.9 us
    ppermute x16, waiting for transfers between devices, shifted(): return lax.ppermute(value, axis, pairs)  26.8 us
    ppermute x16, starting transfers between devices, shifted(): return lax.ppermute(value, axis, pairs)  26.2 us
    unnamed x136, local copies, waits for them, and re-layouts  20.8 us
    reduce_sum x1, other arithmetic, on_device(): jnp.sum(lax.all_gather(encode_grads, ('face', 'sub')), axis=0)  16.4 us
  transfers between devices with their start and end apart: 20, of which 7 were waited for; matrix products, arithmetic and copies ran while one was open for 6% of the time, Pallas kernels for 0%

profile of v1, /device:TPU:0, one launch (start us, length us, event | category | flops | bytes accessed | tf_op | source)
XLA Modules:
  0.0 588.4 jit_solution(15938592925978682079)
XLA Ops:
  8.0 2.4 constant_dynamic-update-slice_fusion.4
  12.2 2.5 collective-permute-start.3
  14.6 4.6 collective-permute-start.1
  19.2 3.1 fusion.81
  24.0 6.8 %collective-permute-done = bf16[256,512]{1,0:T(8,128)(2,1)S(1)} collective-permute-done((bf16[256,512]{1,0:T(8,128)(2,1)}, bf16[256,512]{1,0:T(8,128)(2,1)S(1)}, u32[]{:S(2)}, u32[]{:S(2)}) %collective-permute-start) | collective-permute-done | bytes 262176 | tf_op jit(solution)/shard_map/ppermute | solution.py:12
  35.6 3.6 fusion.3
  39.2 2.3 fusion.146
  50.1 5.0 all-to-all-start
  56.6 4.3 collective-permute-start.5
  70.3 3.0 fusion.17
  73.3 2.3 fusion.147
  82.4 2.1 convolution_add_fusion.4
  84.5 4.3 fusion.141
  88.9 2.9 multiply_convert_fusion.4
  91.9 2.7 multiply_convert_fusion.3
  94.6 2.6 fusion.151
  98.7 5.1 collective-permute-start.8
  106.0 2.6 all-to-all-start.1
  112.0 5.6 collective-permute-done.9
  131.0 2.1 multiply_convert_fusion.2
  133.2 6.9 %fusion.152 = (bf16[1664,512]{1,0:T(8,128)(2,1)S(1)}, f32[1664,512]{1,0:T(8,128)}) fusion(f32[1024,512]{1,0:T(8,128)} %copy-done.57, bf16[1024,512]{0,1:T(8,128)(2,1)S(1)} %multiply_convert_fusion.2, bf16[10,512,512]{2,1,0:T(8,128)(2,1)} %param.26, s32[1024]{0:T(1024)S(1)} %copy-done.32, s32[1024]{0:T(1024)S(1)} %copy-done.50), kind=kOutput, calls=%fused_computation.225 | convolution fusion | flops 2292383744 | bytes 8790016 | tf_op jit(solution)/shard_map/dot_general | solution.py:42
  146.1 7.9 %collective-permute-done.12 = bf16[256,512]{1,0:T(8,128)(2,1)S(1)} collective-permute-done((bf16[256,512]{1,0:T(8,128)(2,1)S(1)}, bf16[256,512]{1,0:T(8,128)(2,1)S(1)}, u32[]{:S(2)}, u32[]{:S(2)}) %collective-permute-start.12) | collective-permute-done | bytes 262176 | tf_op jit(solution)/shard_map/ppermute | solution.py:12
  154.0 5.5 collective-permute-done.13
  159.5 2.3 fusion.28
  163.2 109.5 %all-reduce.2.cloned.1.call-done = bf16[7,512,512]{1,2,0:T(8,128)(2,1)} async-done(((bf16[7,512,512]{1,2,0:T(8,128)(2,1)}), bf16[7,512,512]{1,2,0:T(8,128)(2,1)}) %all-reduce.2.cloned.1.call-update) | async-done | bytes 3670032 | tf_op jit(solution)/shard_map/psum | solution.py:214
  274.3 2.1 fusion.10
  277.7 2.1 fusion.48
  279.8 2.3 convolution_convert_fusion.1
  282.1 268.3 %all-gather.3.cloned.1.call-done = bf16[96,512,512]{2,1,0:T(8,128)(2,1)} async-done(((bf16[3,512,512]{2,1,0:T(8,128)(2,1)}), bf16[96,512,512]{2,1,0:T(8,128)(2,1)}) %all-gather.3.cloned.1.call-update) | async-done | bytes 50331664 | tf_op jit(solution)/shard_map/all_gather | solution.py:230
  550.4 16.4 %reduce_sum.156 = bf16[3,512,512]{2,1,0:T(8,128)(2,1)S(1)} reduce(bf16[32,3,512,512]{3,2,1,0:T(8,128)(2,1)} %bitcast.143, bf16[]{:T(256)} %constant.35.clone.1), dimensions={0}, to_apply=%region_13.14 | reduce | flops 24379392 | bytes 51904512 | tf_op jit(solution)/shard_map/reduce_sum | solution.py:230
  567.5 6.0 %multiply_convert_fusion = bf16[10,512,512]{1,2,0:T(8,128)(2,1)} fusion(bf16[7,512,512]{1,2,0:T(8,128)(2,1)} %all-reduce.2.cloned.1.call-done, bf16[3,512,512]{1,2,0:T(8,128)(2,1)S(1)} %copy.67, f32[10]{0:T(128)S(1)} %copy-done.45), kind=kLoop, calls=%fused_computation | loop fusion | flops 10485760 | bytes 10485800 | tf_op jit(solution)/shard_map/convert_element_type | solution.py:235
  573.6 8.0 %copy.69 = bf16[10,512,512]{2,1,0:T(8,128)(2,1)} copy(bf16[10,512,512]{1,2,0:T(8,128)(2,1)} %multiply_convert_fusion) | data formatting | bytes 10485760
  (224 shorter events, 66.4 us)
Async XLA Ops:
  7.2 12.0 %copy-start = (bf16[1024,512]{1,0:T(8,128)(2,1)S(1)}, bf16[1024,512]{1,0:T(8,128)(2,1)}, u32[]{:S(2)}) copy-start(bf16[1024,512]{1,0:T(8,128)(2,1)} %param.16) | copy-start | bytes 3145732
  12.2 10.4 %copy-start.10 = (bf16[1024,512]{1,0:T(8,128)(2,1)S(1)}, bf16[1024,512]{1,0:T(8,128)(2,1)}, u32[]{:S(2)}) copy-start(bf16[1024,512]{1,0:T(8,128)(2,1)} %param.18) | copy-start | bytes 3145732
  12.2 20.8 %collective-permute-start.3 = (bf16[256,512]{1,0:T(8,128)(2,1)}, bf16[256,512]{1,0:T(8,128)(2,1)S(1)}, u32[]{:S(2)}, u32[]{:S(2)}) collective-permute-start(bf16[256,512]{1,0:T(8,128)(2,1)} %get-tuple-element.39), channel_id=1, source_target_pairs={{0,24},{8,0},{16,8},{24,16},{1,25},{9,1},{17,9},{25,17},{2,26},{10... | collective-permute-start | bytes 786440 | tf_op jit(solution)/shard_map/ppermute | solution.py:12
  14.6 17.6 %collective-permute-start.2 = (bf16[256,512]{1,0:T(8,128)(2,1)}, bf16[256,512]{1,0:T(8,128)(2,1)S(1)}, u32[]{:S(2)}, u32[]{:S(2)}) collective-permute-start(bf16[256,512]{1,0:T(8,128)(2,1)} %get-tuple-element.40), channel_id=1, source_target_pairs={{0,8},{8,16},{16,24},{24,0},{1,9},{9,17},{17,25},{25,1},{2,10},{10... | collective-permute-start | bytes 786440 | tf_op jit(solution)/shard_map/ppermute | solution.py:12
  14.6 16.9 %collective-permute-start.1 = (bf16[256,512]{1,0:T(8,128)(2,1)}, bf16[256,512]{1,0:T(8,128)(2,1)S(1)}, u32[]{:S(2)}, u32[]{:S(2)}) collective-permute-start(bf16[256,512]{1,0:T(8,128)(2,1)} %get-tuple-element.41), channel_id=1, source_target_pairs={{0,7},{1,0},{2,1},{3,2},{4,3},{5,4},{6,5},{7,6},{8,15},{9,8},{10,9... | collective-permute-start | bytes 786440 | tf_op jit(solution)/shard_map/ppermute | solution.py:12
  19.2 11.6 %collective-permute-start = (bf16[256,512]{1,0:T(8,128)(2,1)}, bf16[256,512]{1,0:T(8,128)(2,1)S(1)}, u32[]{:S(2)}, u32[]{:S(2)}) collective-permute-start(bf16[256,512]{1,0:T(8,128)(2,1)} %get-tuple-element.42), channel_id=1, source_target_pairs={{0,1},{1,2},{2,3},{3,4},{4,5},{5,6},{6,7},{7,0},{8,9},{9,10},{10,1... | collective-permute-start | bytes 786440 | tf_op jit(solution)/shard_map/ppermute | solution.py:12
  19.2 16.4 %copy-start.31 = (s32[1024]{0:T(1024)}, s32[1024]{0:T(1024)S(1)}, u32[]{:S(2)}) copy-start(s32[1024]{0:T(1024)S(1)} %broadcast_add_fusion.1) | copy-start | bytes 12292
  22.3 48.0 %copy-start.33 = (s32[1024]{0:T(1024)}, s32[1024]{0:T(1024)S(1)}, u32[]{:S(2)}) copy-start(s32[1024]{0:T(1024)S(1)} %broadcast_add_fusion) | copy-start | bytes 12292
  22.6 21.9 %copy-start.27 = (s32[384]{0:T(512)}, s32[384]{0:T(512)S(1)}, u32[]{:S(2)}) copy-start(s32[384]{0:T(512)S(1)} %pad_add_fusion) | copy-start | bytes 4612
  22.6 11.1 %copy-start.16 = (bf16[128,512]{1,0:T(8,128)(2,1)S(1)}, bf16[128,512]{1,0:T(8,128)(2,1)}, u32[]{:S(2)}) copy-start(bf16[128,512]{1,0:T(8,128)(2,1)} %param.15) | copy-start | bytes 393220
  22.6 13.0 %copy-start.49 = (s32[1024]{0:T(1024)S(1)}, s32[1024]{0:T(1024)}, u32[]{:S(2)}) copy-start(s32[1024]{0:T(1024)} %param.20) | copy-start | bytes 12292
  44.8 25.5 %copy-start.47 = (s32[1024]{0:T(1024)S(1)}, s32[1024]{0:T(1024)}, u32[]{:S(2)}) copy-start(s32[1024]{0:T(1024)} %param.24) | copy-start | bytes 12292
  45.5 15.3 %collective-permute-start.4 = (bf16[64,512]{1,0:T(8,128)(2,1)}, bf16[64,512]{1,0:T(8,128)(2,1)}, u32[]{:S(2)}, u32[]{:S(2)}) collective-permute-start(bf16[64,512]{1,0:T(8,128)(2,1)} %get-tuple-element.50), channel_id=1, source_target_pairs={{0,1},{1,2},{2,3},{3,4},{4,5},{5,6},{6,7},{7,0},{8,9},{9,10},{10,1... | collective-permute-start | bytes 196616 | tf_op jit(solution)/shard_map/ppermute | solution.py:12
  50.1 15.1 %all-to-all-start = ((bf16[32,4,512]{2,1,0:T(4,128)(2,1)}), bf16[32,4,512]{2,1,0:T(4,128)(2,1)}, u32[]{:S(2)}, u32[]{:S(2)}) async-start(bf16[32,4,512]{2,1,0:T(4,128)(2,1)} %reshape.127), calls=%async_computation | async-start | bytes 262144 | tf_op jit(solution)/shard_map/all_to_all | solution.py:93
  55.1 9.5 %collective-permute-start.7 = (bf16[64,512]{1,0:T(8,128)(2,1)}, bf16[64,512]{1,0:T(8,128)(2,1)S(1)}, u32[]{:S(2)}, u32[]{:S(2)}) collective-permute-start(bf16[64,512]{1,0:T(8,128)(2,1)} %get-tuple-element.47), channel_id=1, source_target_pairs={{0,24},{8,0},{16,8},{24,16},{1,25},{9,1},{17,9},{25,17},{2,26},{10... | collective-permute-start | bytes 196616 | tf_op jit(solution)/shard_map/ppermute | solution.py:12
  56.6 7.4 %collective-permute-start.6 = (bf16[64,512]{1,0:T(8,128)(2,1)}, bf16[64,512]{1,0:T(8,128)(2,1)S(1)}, u32[]{:S(2)}, u32[]{:S(2)}) collective-permute-start(bf16[64,512]{1,0:T(8,128)(2,1)} %get-tuple-element.48), channel_id=1, source_target_pairs={{0,8},{8,16},{16,24},{24,0},{1,9},{9,17},{17,25},{25,1},{2,10},{10... | collective-permute-start | bytes 196616 | tf_op jit(solution)/shard_map/ppermute | solution.py:12
  56.6 6.8 %collective-permute-start.5 = (bf16[64,512]{1,0:T(8,128)(2,1)}, bf16[64,512]{1,0:T(8,128)(2,1)S(1)}, u32[]{:S(2)}, u32[]{:S(2)}) collective-permute-start(bf16[64,512]{1,0:T(8,128)(2,1)} %get-tuple-element.49), channel_id=1, source_target_pairs={{0,7},{1,0},{2,1},{3,2},{4,3},{5,4},{6,5},{7,6},{8,15},{9,8},{10,9... | collective-permute-start | bytes 196616 | tf_op jit(solution)/shard_map/ppermute | solution.py:12
  98.7 19.1 %copy-start.28 = (s32[384]{0:T(512)S(1)}, s32[384]{0:T(512)}, u32[]{:S(2)}) copy-start(s32[384]{0:T(512)} %copy-done.27) | copy-start | bytes 4612
  98.7 13.3 %collective-permute-start.8 = (bf16[64,512]{1,0:T(8,128)(2,1)S(1)}, bf16[64,512]{1,0:T(8,128)(2,1)S(1)}, u32[]{:S(2)}, u32[]{:S(2)}) collective-permute-start(bf16[64,512]{1,0:T(8,128)(2,1)S(1)} %get-tuple-element.46), channel_id=1, source_target_pairs={{0,7},{1,0},{2,1},{3,2},{4,3},{5,4},{6,5},{7,6},{8,15},{9,8},{10,9... | collective-permute-start | bytes 196616 | tf_op jit(solution)/shard_map/ppermute | solution.py:12
  105.2 15.2 %copy-start.26 = (s32[1024]{0:T(1024)S(1)}, s32[1024]{0:T(1024)}, u32[]{:S(2)}) copy-start(s32[1024]{0:T(1024)} %param.21) | copy-start | bytes 12292
  106.0 11.8 %all-to-all-start.1 = ((bf16[32,4,512]{2,1,0:T(4,128)(2,1)}), bf16[32,4,512]{2,1,0:T(4,128)(2,1)S(1)}, u32[]{:S(2)}, u32[]{:S(2)}) async-start(bf16[32,4,512]{2,1,0:T(4,128)(2,1)} %reshape.129), calls=%async_computation.1 | async-start | bytes 262144 | tf_op jit(solution)/shard_map/all_to_all | solution.py:97
  108.5 164.1 %all-reduce.2.cloned.1.call-start = ((), (), s32[]{:S(2)}) async-start(), calls=%async_computation.2 | async-start | bytes 7340032 | tf_op jit(solution)/shard_map/psum | solution.py:214
  108.6 9.1 %collective-permute-start.11 = (bf16[64,512]{1,0:T(8,128)(2,1)S(1)}, bf16[64,512]{1,0:T(8,128)(2,1)S(1)}, u32[]{:S(2)}, u32[]{:S(2)}) collective-permute-start(bf16[64,512]{1,0:T(8,128)(2,1)S(1)} %get-tuple-element.43), channel_id=1, source_target_pairs={{0,8},{8,16},{16,24},{24,0},{1,9},{9,17},{17,25},{25,1},{2,10},{10... | collective-permute-start | bytes 196616 | tf_op jit(solution)/shard_map/ppermute | solution.py:12
  108.7 8.9 %collective-permute-start.10 = (bf16[64,512]{1,0:T(8,128)(2,1)S(1)}, bf16[64,512]{1,0:T(8,128)(2,1)S(1)}, u32[]{:S(2)}, u32[]{:S(2)}) collective-permute-start(bf16[64,512]{1,0:T(8,128)(2,1)S(1)} %get-tuple-element.44), channel_id=1, source_target_pairs={{0,24},{8,0},{16,8},{24,16},{1,25},{9,1},{17,9},{25,17},{2,26},{10... | collective-permute-start | bytes 196616 | tf_op jit(solution)/shard_map/ppermute | solution.py:12
  110.4 7.3 %collective-permute-start.9 = (bf16[64,512]{1,0:T(8,128)(2,1)S(1)}, bf16[64,512]{1,0:T(8,128)(2,1)S(1)}, u32[]{:S(2)}, u32[]{:S(2)}) collective-permute-start(bf16[64,512]{1,0:T(8,128)(2,1)S(1)} %get-tuple-element.45), channel_id=1, source_target_pairs={{0,1},{1,2},{2,3},{3,4},{4,5},{5,6},{6,7},{7,0},{8,9},{9,10},{10,1... | collective-permute-start | bytes 196616 | tf_op jit(solution)/shard_map/ppermute | solution.py:12
  130.9 419.5 %all-gather.3.cloned.1.call-start = ((), (), s32[]{:S(2)}) async-start(), calls=%async_computation.3 | async-start | bytes 51904512 | tf_op jit(solution)/shard_map/all_gather | solution.py:230
  140.2 13.8 %collective-permute-start.12 = (bf16[256,512]{1,0:T(8,128)(2,1)S(1)}, bf16[256,512]{1,0:T(8,128)(2,1)S(1)}, u32[]{:S(2)}, u32[]{:S(2)}) collective-permute-start(bf16[256,512]{1,0:T(8,128)(2,1)S(1)} %get-tuple-element.35), channel_id=1, source_target_pairs={{0,7},{1,0},{2,1},{3,2},{4,3},{5,4},{6,5},{7,6},{8,15},{9,8},{10,9... | collective-permute-start | bytes 786440 | tf_op jit(solution)/shard_map/ppermute | solution.py:12
  141.6 12.3 %collective-permute-start.15 = (bf16[256,512]{1,0:T(8,128)(2,1)S(1)}, bf16[256,512]{1,0:T(8,128)(2,1)S(1)}, u32[]{:S(2)}, u32[]{:S(2)}) collective-permute-start(bf16[256,512]{1,0:T(8,128)(2,1)S(1)} %get-tuple-element.36), channel_id=1, source_target_pairs={{0,8},{8,16},{16,24},{24,0},{1,9},{9,17},{17,25},{25,1},{2,10},{10... | collective-permute-start | bytes 786440 | tf_op jit(solution)/shard_map/ppermute | solution.py:12
  141.6 12.3 %collective-permute-start.14 = (bf16[256,512]{1,0:T(8,128)(2,1)S(1)}, bf16[256,512]{1,0:T(8,128)(2,1)S(1)}, u32[]{:S(2)}, u32[]{:S(2)}) collective-permute-start(bf16[256,512]{1,0:T(8,128)(2,1)S(1)} %get-tuple-element.37), channel_id=1, source_target_pairs={{0,24},{8,0},{16,8},{24,16},{1,25},{9,1},{17,9},{25,17},{2,26},{10... | collective-permute-start | bytes 786440 | tf_op jit(solution)/shard_map/ppermute | solution.py:12
  143.4 16.1 %copy-start.30 = (s32[1,2,4,128]{3,1,2,0:T(2,128)S(1)}, s32[1,2,4,128]{3,1,2,0:T(2,128)}, u32[]{:S(2)}) copy-start(s32[1,2,4,128]{3,1,2,0:T(2,128)} %copy-done.29) | copy-start | bytes 12292
  143.4 16.1 %collective-permute-start.13 = (bf16[256,512]{1,0:T(8,128)(2,1)S(1)}, bf16[256,512]{1,0:T(8,128)(2,1)S(1)}, u32[]{:S(2)}, u32[]{:S(2)}) collective-permute-start(bf16[256,512]{1,0:T(8,128)(2,1)S(1)} %get-tuple-element.38), channel_id=1, source_target_pairs={{0,1},{1,2},{2,3},{3,4},{4,5},{5,6},{6,7},{7,0},{8,9},{9,10},{10,1... | collective-permute-start | bytes 786440 | tf_op jit(solution)/shard_map/ppermute | solution.py:12
  163.2 111.1 %copy-start.3 = (bf16[1024,512]{0,1:T(8,128)(2,1)S(1)}, bf16[1024,512]{0,1:T(8,128)(2,1)}, u32[]{:S(2)}) copy-start(bf16[1024,512]{0,1:T(8,128)(2,1)} %copy.57) | copy-start | bytes 3145732
  (47 other events, 196.5 us)
Sparse Core Ops, SparseCore 0:
  131.0 141.5 all-reduce.1
  276.2 274.2 all-gather.2
